TPU v7x, 32 devices: a whole 2x2x4 slice. The times are simulated.
32 devices in a mesh: grp: 4 (over z), tp: 4 (over y, x), rep: 2 (over core).
Axes of the slice: x: 2, y: 2, z: 4, core: 2. Of those that a mesh axis runs over, the one named last changes fastest.
Arguments:
- query_rows: bfloat16 [4, 1024, 2048], P('tp', ('grp', 'rep')), may hold values from -120 to 120
- key_rows: bfloat16 [4, 1024, 512], P('tp', ('grp', 'rep')), may hold values from -6 to 6, as said below
- value_rows: bfloat16 [4, 1024, 512], P('tp', ('grp', 'rep')), may hold values from -6 to 6
- teacher_codes: bfloat16 [4, 1024, 4096], P(None, ('grp', 'rep'), 'tp'), may hold values from -6 to 6
- teacher_scales: bfloat16 [4, 1024, 32], P(None, ('grp', 'rep'), 'tp'), may hold values from 0.099609375 to 1
- projection: bfloat16 [2048, 4096], P(None, ('grp', 'rep')), may hold values from -0.125 to 0.125
Outputs:
- grad_query: bfloat16 [4, 1024, 2048], P('tp', ('grp', 'rep'))
- grad_key: bfloat16 [4, 1024, 512], P('tp', ('grp', 'rep'))
- grad_value: bfloat16 [4, 1024, 512], P('tp', ('grp', 'rep'))
Inputs may be any that keep to these rules, and one draw needn't show every extreme that they name: `key_rows`: keys of every head.
All inputs are finite; a program needn't handle non-finite values.
Results may differ from a plain program's by a relative error of at most 0.014.
Values may be sent and summed in bfloat16 or wider, within the bound.
A program may use at most 128 MiB of HBM per device.

v0:
```python
import math

import jax
import jax.numpy as jnp
from jax import lax
from jax.sharding import PartitionSpec as P

HEADS = 16
KV_HEADS = 4
HEAD_DIM = 128
QBLOCK = 128


masked_low = -1e30


def shards(query_rows, key_rows, value_rows, teacher_codes, teacher_scales, projection):
    rows_dev = query_rows.shape[1]
    group_size = HEADS // KV_HEADS
    inv_root = 1.0 / math.sqrt(HEAD_DIM)
    keys_all, values_all = (
        lax.all_gather(key_rows, ("grp", "rep"), axis=1, tiled=True),
        lax.all_gather(value_rows, ("grp", "rep"), axis=1, tiled=True),
    )
    length = keys_all.shape[1]
    key_block = min(1024, length)
    my_index = lax.axis_index(("grp", "rep"))
    first_row = my_index * rows_dev
    needed = (first_row + rows_dev + key_block - 1) // key_block
    queries = query_rows[0].reshape(rows_dev, KV_HEADS, group_size, HEAD_DIM).transpose(1, 2, 0, 3)
    key_heads = keys_all[0].reshape(length, KV_HEADS, HEAD_DIM).transpose(1, 0, 2)
    value_heads = values_all[0].reshape(length, KV_HEADS, HEAD_DIM).transpose(1, 0, 2)
    row_pos = first_row + jnp.arange(rows_dev, dtype=jnp.int32)
    slab_codes, slab_scales = (
        lax.all_to_all(teacher_codes, "tp", split_axis=0, concat_axis=2, tiled=True),
        lax.all_to_all(teacher_scales, "tp", split_axis=0, concat_axis=2, tiled=True),
    )

    def block_scores(block_index):
        offset = block_index * key_block
        raw_scores = (
            jnp.einsum("hgqd,hkd->hgqk", queries, key_heads, preferred_element_type=jnp.float32)
            * inv_root
        )
        col_pos = offset + jnp.arange(key_block, dtype=jnp.int32)
        allowed = col_pos[None, :] <= row_pos[:, None]
        return (jnp.where(allowed, raw_scores, masked_low), key_heads, value_heads)

    def stats_step(block_index, running):
        row_peak, row_total = running
        scores, key_part, value_part = block_scores(block_index)
        new_peak = jnp.maximum(row_peak, scores.max(-1))
        row_total = row_total * jnp.exp(row_peak - new_peak) + jnp.exp(
            scores - new_peak[..., None]
        ).sum(-1)
        return (new_peak, row_total)

    stat_shape = (KV_HEADS, group_size, rows_dev)
    row_peak, row_total = lax.fori_loop(
        0,
        needed,
        stats_step,
        (jnp.full(stat_shape, masked_low, jnp.float32), jnp.zeros(stat_shape, jnp.float32)),
    )

    def block_probs(scores):
        return jnp.exp(scores - row_peak[..., None]) / row_total[..., None]

    def output_step(block_index, running):
        scores, key_part, value_part = block_scores(block_index)
        prob_low = block_probs(scores).astype(jnp.bfloat16)
        return running + jnp.einsum(
            "hgqk,hkd->hgqd", prob_low, value_part, preferred_element_type=jnp.float32
        )

    attn_wide = lax.fori_loop(
        0, needed, output_step, jnp.zeros((KV_HEADS, group_size, rows_dev, HEAD_DIM), jnp.float32)
    )
    attn_low = (
        attn_wide.transpose(2, 0, 1, 3).reshape(rows_dev, HEADS * HEAD_DIM).astype(jnp.bfloat16)
    )
    col_width = projection.shape[1]
    shard_piece = lax.all_gather(projection, ("grp", "rep"), axis=1, tiled=True)
    pieces = shard_piece.shape[1] // col_width
    shaped = shard_piece.reshape(shard_piece.shape[0], pieces, col_width)
    approx = jnp.einsum("td,dsc->tsc", attn_low, shaped, preferred_element_type=jnp.float32)
    code_rows = slab_codes[0].astype(jnp.float32)
    scale_rows = slab_scales[0].astype(jnp.float32)
    target = (code_rows.reshape(rows_dev, -1, QBLOCK) * scale_rows[..., None]).reshape(
        rows_dev, pieces, col_width
    )
    errors = (approx - target).astype(jnp.bfloat16)
    partial_terms = jnp.einsum(
        "tsc,dsc->std", errors, shaped, preferred_element_type=jnp.float32
    ).astype(jnp.bfloat16)
    grad_attn = partial_terms.astype(jnp.float32).sum(0)
    grad_low = grad_attn.astype(jnp.bfloat16)
    grad_heads = grad_low.reshape(rows_dev, KV_HEADS, group_size, HEAD_DIM).transpose(1, 2, 0, 3)
    row_delta = (grad_heads.astype(jnp.float32) * attn_wide).sum(-1)

    def back_step(block_index, running):
        grad_queries, grad_keys, grad_values = running
        scores, key_part, value_part = block_scores(block_index)
        probs = block_probs(scores)
        prob_low = probs.astype(jnp.bfloat16)
        grad_prob = jnp.einsum(
            "hgqd,hkd->hgqk", grad_heads, value_part, preferred_element_type=jnp.float32
        )
        grad_score = (probs * (grad_prob - row_delta[..., None]) * inv_root).astype(jnp.bfloat16)
        grad_queries = grad_queries + jnp.einsum(
            "hgqk,hkd->hgqd", grad_score, key_part, preferred_element_type=jnp.float32
        )
        key_piece = jnp.einsum(
            "hgqk,hgqd->hkd", grad_score, queries, preferred_element_type=jnp.float32
        )
        value_piece = jnp.einsum(
            "hgqk,hgqd->hkd", prob_low, grad_heads, preferred_element_type=jnp.float32
        )
        grad_keys = key_piece
        grad_values = value_piece
        return (grad_queries, grad_keys, grad_values)

    zeros_kv = jnp.zeros((KV_HEADS, length, HEAD_DIM), jnp.float32)
    grad_queries, grad_keys, grad_values = lax.fori_loop(
        0,
        needed,
        back_step,
        (jnp.zeros((KV_HEADS, group_size, rows_dev, HEAD_DIM), jnp.float32), zeros_kv, zeros_kv),
    )
    key_terms = grad_keys.transpose(1, 0, 2).reshape(1, length, KV_HEADS * HEAD_DIM)
    value_terms = grad_values.transpose(1, 0, 2).reshape(1, length, KV_HEADS * HEAD_DIM)
    key_grad, value_grad = (
        lax.psum_scatter(
            key_terms.astype(jnp.bfloat16), ("grp", "rep"), scatter_dimension=1, tiled=True
        ).astype(jnp.float32),
        lax.psum_scatter(
            value_terms.astype(jnp.bfloat16), ("grp", "rep"), scatter_dimension=1, tiled=True
        ).astype(jnp.float32),
    )
    query_grad = (
        grad_queries.transpose(2, 0, 1, 3)
        .reshape(1, rows_dev, HEADS * HEAD_DIM)
        .astype(jnp.bfloat16)
    )
    return (query_grad, key_grad.astype(jnp.bfloat16), value_grad.astype(jnp.bfloat16))


def solution(mesh):
    placed = (
        P("tp", ("grp", "rep"), None),
        P("tp", ("grp", "rep"), None),
        P("tp", ("grp", "rep"), None),
        P(None, ("grp", "rep"), "tp"),
        P(None, ("grp", "rep"), "tp"),
        P(None, ("grp", "rep")),
    )
    return jax.shard_map(
        shards,
        mesh=mesh,
        in_specs=placed,
        out_specs=(
            P("tp", ("grp", "rep"), None),
            P("tp", ("grp", "rep"), None),
            P("tp", ("grp", "rep"), None),
        ),
        check_vma=False,
    )
```

profile of v0, /device:TPU:0, one launch (start us, length us, event | category | flops | bytes accessed | tf_op | source)
XLA Modules:
  0.0 326.8 jit_solution(2066689042145613132)
XLA Ops:
  10.7 4.0 %copy.49 = bf16[2048,512]{0,1:T(8,128)(2,1)} copy(bf16[2048,512]{1,0:T(8,128)(2,1)} %param.17) | data formatting | bytes 4194304 | tf_op args[5]
  14.7 5.2 %all-to-all-start.1 = ((bf16[4,128,8]{1,2,0:T(8,128)(2,1)}), bf16[4,128,8]{1,2,0:T(8,128)(2,1)S(1)}, u32[]{:S(2)}, u32[]{:S(2)}) async-start(bf16[4,128,8]{1,2,0:T(8,128)(2,1)} %param.16), calls=%async_computation.1 | async-start | bytes 16384 | tf_op jit(solution)/shard_map/all_to_all | solution.py:36
  19.9 2.3 copy.52
  22.2 2.4 all-to-all-done.1
  24.6 4.2 %all-to-all-start = ((bf16[4,128,1024]{1,2,0:T(8,128)(2,1)}), bf16[4,128,1024]{1,2,0:T(8,128)(2,1)}, u32[]{:S(2)}, u32[]{:S(2)}) async-start(bf16[4,128,1024]{1,2,0:T(8,128)(2,1)} %copy.52), calls=%async_computation | async-start | bytes 2097152 | tf_op jit(solution)/shard_map/all_to_all | solution.py:35
  29.7 1.8 copy.54
  31.5 9.9 %all-to-all-done = bf16[4,128,1024]{1,2,0:T(8,128)(2,1)} async-done(((bf16[4,128,1024]{1,2,0:T(8,128)(2,1)}), bf16[4,128,1024]{1,2,0:T(8,128)(2,1)}, u32[]{:S(2)}, u32[]{:S(2)}) %all-to-all-start) | async-done | bytes 1048608 | tf_op jit(solution)/shard_map/all_to_all | solution.py:35
  42.8 1.8 copy.53
  46.2 15.4 %all-gather.6.cloned.1.call-done = bf16[1,1024,512]{1,2,0:T(8,128)(2,1)} async-done(((bf16[1,128,512]{1,2,0:T(8,128)(2,1)}), bf16[1,1024,512]{1,2,0:T(8,128)(2,1)}) %all-gather.6.cloned.1.call-update) | async-done | bytes 1048592 | tf_op jit(solution)/shard_map/all_gather | solution.py:23
  63.3 4.2 %while.39 = (s32[]{:T(128)}, f32[4,4,128]{2,1,0:T(4,128)S(1)}, f32[4,4,128]{2,1,0:T(4,128)S(1)}, s32[]{:T(128)}, bf16[4,4,128,128]{3,2,1,0:T(8,128)(2,1)S(1)}, /...) while((s32[]{:T(128)}, f32[4,4,128]{2,1,0:T(4,128)S(1)}, ...), condition=%wide.region_3.4_spmd.clone, body=%wide.region_0.3_spmd.clone.sunk | while | flops 551687296 | bytes 18859120 | solution.py:59
  65.1 2.3 exponential_reduce_fusion.2
  68.6 5.9 %while.40 = (s32[]{:T(128)}, f32[4,4,128,128]{3,2,1,0:T(8,128)}, s32[]{:T(128)}, bf16[4,4,128,128]{3,2,1,0:T(8,128)(2,1)S(1)}, bf16[4,1024,128]{2,1,0:T(8,128)(2...) while((s32[]{:T(128)}, f32[4,4,128,128]{3,2,1,0:T(8,128)}, ...), condition=%wide.region_5.6_spmd.clone, body=%wide.region_4.5_spmd.clone.sunk | while | flops 1084621952 | bytes 5006465 | solution.py:76
  68.7 5.8 %fusion.68 = f32[4,4,128,128]{3,2,1,0:T(8,128)} fusion(f32[4,4,128,128]{3,2,1,0:T(8,128)} %get-tuple-element.569, f32[4,4,128]{2,1,0:T(4,128)S(1)} %get-tuple-element.585, f32[4,4,128]{2,1,0:T(4,128)S(1)} %get-tuple-element.584, pred[128,1024]{1,0:T(8,128)(4,1)S(1)} %broadcast_compare_fusion.7, bf16[4,4,128,128]{3,2,1,0:T(8,128)(2,1)S(1)} %get-tuple-element.582, ...), kind=kOutput, calls=%fused_computation.15.clone.1 | convolution fusion | flops 1084489728 | bytes 4866048 | tf_op jit(solution)/shard_map/while/body/hgqk,hkd->hgqd/dot_general | solution.py:72
  74.5 3.0 copy.48
  78.9 134.2 %all-gather.8.cloned.1.call-done = bf16[2048,4096]{0,1:T(8,128)(2,1)} async-done(((bf16[2048,512]{0,1:T(8,128)(2,1)}), bf16[2048,4096]{0,1:T(8,128)(2,1)}) %all-gather.8.cloned.1.call-update) | async-done | bytes 16777232 | tf_op jit(solution)/shard_map/all_gather | solution.py:83
  213.1 21.9 %convert_reduce_fusion = bf16[128,2048]{1,0:T(8,128)(2,1)} fusion(bf16[2048,8,512]{0,2,1:T(8,128)(2,1)} %bitcast.144, f32[128,8,512]{2,0,1:T(8,128)} %copy.53, f32[128,8,512]{2,0,1:T(8,128)} %copy.54, bf16[128,2048,1]{0,1,2:T(8,128)(2,1)S(1)} %bitcast.147), kind=kOutput, calls=%fused_computation.36 | convolution fusion | flops 4300472320 | bytes 22020096 | tf_op jit(solution)/shard_map/tsc,dsc->std/dot_general | solution.py:93
  241.6 11.0 %while.41 = (s32[]{:T(128)}, f32[4,4,128,128]{3,2,1,0:T(8,128)S(1)}, bf16[4,1024,128]{2,1,0:T(8,128)(2,1)}, bf16[4,1024,128]{2,1,0:T(8,128)(2,1)}, s32[]{:T(128)...) while((s32[]{:T(128)}, ...), condition=%wide.region_9.10_spmd.clone, body=%wide.region_8.9_spmd.clone.sunk | while | flops 2703623168 | bytes 51676348 | solution.py:124
  241.7 2.8 exponential_divide_fusion.2
  247.3 2.6 convolution_bitcast_fusion.2
  249.9 2.6 fusion.79
  252.5 2.0 copy.63
  255.8 2.0 copy.64
  260.8 26.0 %reduce-scatter.3.cloned.1.call-done = bf16[1,128,512]{2,1,0:T(8,128)(2,1)} async-done(((bf16[1,1024,512]{2,1,0:T(8,128)(2,1)}), bf16[1,128,512]{2,1,0:T(8,128)(2,1)}) %reduce-scatter.3.cloned.1.call-update) | async-done | bytes 131088 | tf_op jit(solution)/shard_map/reduce_scatter | solution.py:133
  286.8 33.4 %reduce-scatter.5.cloned.1.call-done = bf16[1,128,512]{2,1,0:T(8,128)(2,1)} async-done(((bf16[1,1024,512]{2,1,0:T(8,128)(2,1)}), bf16[1,128,512]{2,1,0:T(8,128)(2,1)}) %reduce-scatter.5.cloned.1.call-update) | async-done | bytes 131088 | tf_op jit(solution)/shard_map/reduce_scatter | solution.py:136
  (58 shorter events, 27.0 us)
Async XLA Ops:
  7.2 21.8 %copy-start.3 = (bf16[1,128,2048]{2,1,0:T(8,128)(2,1)S(1)}, bf16[1,128,2048]{2,1,0:T(8,128)(2,1)}, u32[]{:S(2)}) copy-start(bf16[1,128,2048]{2,1,0:T(8,128)(2,1)} %param.12) | copy-start | bytes 1572868
  7.2 37.5 %all-gather.4.cloned.1.call-start = ((), (), s32[]{:S(2)}) async-start(), calls=%async_computation.4 | async-start | bytes 1179648 | tf_op jit(solution)/shard_map/all_gather | solution.py:22
  9.0 52.7 %all-gather.6.cloned.1.call-start = ((), (), s32[]{:S(2)}) async-start(), calls=%async_computation.5 | async-start | bytes 1179648 | tf_op jit(solution)/shard_map/all_gather | solution.py:23
  10.7 202.4 %all-gather.8.cloned.1.call-start = ((), (), s32[]{:S(2)}) async-start(), calls=%async_computation.6 | async-start | bytes 18874368 | tf_op jit(solution)/shard_map/all_gather | solution.py:83
  14.7 9.9 %all-to-all-start.1 = ((bf16[4,128,8]{1,2,0:T(8,128)(2,1)}), bf16[4,128,8]{1,2,0:T(8,128)(2,1)S(1)}, u32[]{:S(2)}, u32[]{:S(2)}) async-start(bf16[4,128,8]{1,2,0:T(8,128)(2,1)} %param.16), calls=%async_computation.1 | async-start | bytes 16384 | tf_op jit(solution)/shard_map/all_to_all | solution.py:36
  24.6 16.8 %all-to-all-start = ((bf16[4,128,1024]{1,2,0:T(8,128)(2,1)}), bf16[4,128,1024]{1,2,0:T(8,128)(2,1)}, u32[]{:S(2)}, u32[]{:S(2)}) async-start(bf16[4,128,1024]{1,2,0:T(8,128)(2,1)} %copy.52), calls=%async_computation | async-start | bytes 2097152 | tf_op jit(solution)/shard_map/all_to_all | solution.py:35
  28.9 258.0 %reduce-scatter.3.cloned.1.call-start = ((), (), s32[]{:S(2)}) async-start(), calls=%async_computation.7 | async-start | bytes 1179648 | tf_op jit(solution)/shard_map/reduce_scatter | solution.py:133
  74.5 160.5 %copy-start = (bf16[4,1024,128]{2,1,0:T(8,128)(2,1)}, bf16[4,1024,128]{2,1,0:T(8,128)(2,1)S(1)}, u32[]{:S(2)}) copy-start(bf16[4,1024,128]{2,1,0:T(8,128)(2,1)S(1)} %get-tuple-element.645) | copy-start | bytes 3145732
  236.3 1.6 copy-start.2
  241.7 2.8 copy-start.1
  255.8 64.4 %reduce-scatter.5.cloned.1.call-start = ((), (), s32[]{:S(2)}) async-start(), calls=%async_computation.8 | async-start | bytes 1179648 | tf_op jit(solution)/shard_map/reduce_scatter | solution.py:136
Sparse Core Ops, SparseCore 0:
  10.1 26.5 all-gather.3
  38.9 22.6 all-gather.5
  63.2 149.8 all-gather.7
  255.9 30.8 reduce-scatter.2
  289.5 30.6 reduce-scatter.4
where the time goes:
time: 328 us; the launch traced here: 327 us
  waiting for transfers between devices  221 us (67%)
  matrix products  40.1 us (12%)
  local copies, waits for them, and re-layouts  34.5 us (11%)
  between operations  14 us (4%)
  starting transfers between devices  9.64 us (3%)
  other arithmetic  7.09 us (2%)
    all_gather x1, waiting for transfers between devices, shards(): shard_piece = lax.all_gather(projection, ('grp', 'rep'), axis=1, tiled=True)  134 us
    reduce_scatter x1, waiting for transfers between devices, shards(): lax.psum_scatter(value_terms.astype(jnp.bfloat16), ('grp', 'rep'), scatte...  33.4 us
    reduce_scatter x1, waiting for transfers between devices, shards(): lax.psum_scatter(key_terms.astype(jnp.bfloat16), ('grp', 'rep'), scatter_...  26 us
    dot_general x1, matrix products, shards(): jnp.einsum('tsc,dsc->std', errors, shaped, preferred_element_type=jnp.flo...  21.9 us
    all_gather x1, waiting for transfers between devices, shards(): lax.all_gather(value_rows, ('grp', 'rep'), axis=1, tiled=True)  15.4 us
    unnamed x15, local copies, waits for them, and re-layouts  14.7 us
    all_to_all x1, waiting for transfers between devices, shards(): lax.all_to_all(teacher_codes, 'tp', split_axis=0, concat_axis=2, tiled=True)  9.92 us
  transfers between devices with their start and end apart: 7, of which 6 were waited for; matrix products, arithmetic and copies ran while one was open for 11% of the time, Pallas kernels for 0%

commit v1 on v0

--- a/solution.py
+++ b/solution.py
@@ -1,8 +1,11 @@
+import functools
 import math
 
 import jax
 import jax.numpy as jnp
 from jax import lax
+from jax.experimental import pallas as pl
+from jax.experimental.pallas import tpu as pltpu
 from jax.sharding import PartitionSpec as P
 
 HEADS = 16
@@ -12,16 +15,148 @@
 
 
 masked_low = -1e30
-
-
-def shards(query_rows, key_rows, value_rows, teacher_codes, teacher_scales, projection):
+QUAD = 4
+CHUNKS = 2
+
+
+def gather_kernel(n_grp, own_ref, all_ref, local_sem, own_sems, z_send, z_recv, x_send, x_recv,
+                  y_send, y_recv, d_send, d_recv, r_send, r_recv):
+    g = lax.axis_index("grp")
+    t = lax.axis_index("tp")
+    r = lax.axis_index("rep")
+    q = lax.rem(t, QUAD)
+    qx = q + 1 - 2 * lax.rem(q, 2)
+    qy = lax.rem(q + 2, QUAD)
+    qd = lax.rem(qx + 2, QUAD)
+    tx = t - q + qx
+    ty = t - q + qy
+    rows = own_ref.shape[0]
+    size = rows // (QUAD * CHUNKS)
+    others = n_grp - 1
+    to_x, to_y, to_r = {"tp": tx}, {"tp": ty}, {"rep": 1 - r}
+    mesh_ids = pl.DeviceIdType.MESH
+
+    barrier = pltpu.get_barrier_semaphore()
+    partners = [{"grp": lax.rem(g + k, n_grp)} for k in range(1, n_grp)] + [to_x, to_y, to_r]
+    for partner in partners:
+        pl.semaphore_signal(barrier, inc=1, device_id=partner, device_id_type=mesh_ids)
+    pl.semaphore_wait(barrier, len(partners))
+
+    def spot(quarter, c):
+        return pl.ds(pl.multiple_of((quarter * CHUNKS + c) * size, size), size)
+
+    def block(k):
+        return lax.rem(g + k, n_grp) * 2 + r
+
+    def sem_at(k, c):
+        return c * others + k - 1
+
+    def send(src, dst, sems, index, to):
+        return pltpu.make_async_remote_copy(
+            src_ref=src, dst_ref=dst, send_sem=sems[0].at[index], recv_sem=sems[1].at[index],
+            device_id=to, device_id_type=mesh_ids)
+
+    def forward(k, c, quarter, sems, index, to):
+        part = all_ref.at[block(k), spot(quarter, c)]
+        return send(part, part, sems, index, to)
+
+    zs, xs, ys, ds, rs = ((z_send, z_recv), (x_send, x_recv), (y_send, y_recv),
+                          (d_send, d_recv), (r_send, r_recv))
+    started = []
+
+    def go(copy):
+        copy.start()
+        started.append(copy)
+
+    order = [1, n_grp - 1] + list(range(2, n_grp - 1)) if n_grp > 2 else [1]
+    events = [(k, c) for c in range(CHUNKS) for k in order]
+    for k, c in events:
+        go(send(own_ref.at[spot(q, c)], all_ref.at[block(0), spot(q, c)], zs, sem_at(k, c),
+                {"grp": lax.rem(g + n_grp - k, n_grp)}))
+    local = pltpu.make_async_copy(own_ref, all_ref.at[block(0)], local_sem.at[0])
+    local.start()
+    own_swap = pltpu.make_async_remote_copy(
+        src_ref=own_ref, dst_ref=all_ref.at[block(0)], send_sem=own_sems.at[0],
+        recv_sem=own_sems.at[1], device_id=to_r, device_id_type=mesh_ids)
+    own_swap.start()
+
+    swaps = []
+
+    def swap(k, c, quarter, lane):
+        copy = forward(k, c, quarter, rs, lane * others * CHUNKS + sem_at(k, c), to_r)
+        go(copy)
+        swaps.append((k, c, (lane, sem_at(k, c))))
+
+    def on_z(k, c):
+        forward(k, c, q, zs, sem_at(k, c), to_x).wait_recv()
+        go(forward(k, c, q, xs, sem_at(k, c), to_x))
+        go(forward(k, c, q, ys, sem_at(k, c), to_y))
+        swap(k, c, q, 0)
+
+    def on_xy(k, c):
+        forward(k, c, qx, xs, sem_at(k, c), to_x).wait_recv()
+        if c % 2 == 0:
+            go(forward(k, c, qx, ds, sem_at(k, c), to_y))
+        swap(k, c, qx, 1)
+        forward(k, c, qy, ys, sem_at(k, c), to_y).wait_recv()
+        if c % 2 == 1:
+            go(forward(k, c, qy, ds, sem_at(k, c), to_x))
+        swap(k, c, qy, 2)
+
+    def on_d(k, c):
+        forward(k, c, qd, ds, sem_at(k, c), to_x).wait_recv()
+        swap(k, c, qd, 3)
+
+    lag = 2
+    for i in range(len(events) + 2 * lag):
+        if i < len(events):
+            on_z(*events[i])
+        if lag <= i < len(events) + lag:
+            on_xy(*events[i - lag])
+        if i >= 2 * lag:
+            on_d(*events[i - 2 * lag])
+
+    local.wait()
+    own_swap.wait_send()
+    for copy in started:
+        copy.wait_send()
+    peer = all_ref.at[lax.rem(g, n_grp) * 2 + 1 - r]
+    pltpu.make_async_remote_copy(
+        src_ref=own_ref, dst_ref=peer, send_sem=own_sems.at[0],
+        recv_sem=own_sems.at[1], device_id=to_r, device_id_type=mesh_ids).wait_recv()
+    for lane, quarter in enumerate((q, qx, qy, qd)):
+        for k, c in events:
+            part = all_ref.at[lax.rem(g + k, n_grp) * 2 + 1 - r, spot(quarter, c)]
+            send(part, part, rs, lane * others * CHUNKS + sem_at(k, c), to_r).wait_recv()
+
+
+def gather_columns(projection, n_grp, n_rep, n_tp):
+    rows, width = projection.shape
+    if n_rep != 2 or n_grp < 2 or n_tp % QUAD or rows % (QUAD * CHUNKS * 16):
+        return lax.all_gather(projection, ("grp", "rep"), axis=0)
+    steps = (n_grp - 1) * CHUNKS
+    dma = pltpu.SemaphoreType.DMA
+    total = n_grp * n_rep * rows * width
+    return pl.pallas_call(
+        functools.partial(gather_kernel, n_grp),
+        out_shape=jax.ShapeDtypeStruct((n_grp * n_rep, rows, width), projection.dtype),
+        in_specs=[pl.BlockSpec(memory_space=pltpu.VMEM)],
+        out_specs=pl.BlockSpec(memory_space=pltpu.HBM),
+        scratch_shapes=[dma((1,)), dma((2,))] + [dma((steps,))] * 8 + [dma((4 * steps,))] * 2,
+        compiler_params=pltpu.CompilerParams(collective_id=0, has_side_effects=True),
+        cost_estimate=pl.CostEstimate(flops=0, bytes_accessed=12 * total, transcendentals=0),
+    )(projection)
+
+
+def shards(mesh, query_rows, key_rows, value_rows, teacher_codes, teacher_scales, projection):
     rows_dev = query_rows.shape[1]
     group_size = HEADS // KV_HEADS
     inv_root = 1.0 / math.sqrt(HEAD_DIM)
-    keys_all, values_all = (
-        lax.all_gather(key_rows, ("grp", "rep"), axis=1, tiled=True),
-        lax.all_gather(value_rows, ("grp", "rep"), axis=1, tiled=True),
-    )
+    kv_width = key_rows.shape[2]
+    pairs_all = lax.all_gather(
+        jnp.concatenate([key_rows, value_rows], 2), ("grp", "rep"), axis=1, tiled=True
+    )
+    keys_all, values_all = pairs_all[..., :kv_width], pairs_all[..., kv_width:]
     length = keys_all.shape[1]
     key_block = min(1024, length)
     my_index = lax.axis_index(("grp", "rep"))
@@ -80,10 +215,11 @@
         attn_wide.transpose(2, 0, 1, 3).reshape(rows_dev, HEADS * HEAD_DIM).astype(jnp.bfloat16)
     )
     col_width = projection.shape[1]
-    shard_piece = lax.all_gather(projection, ("grp", "rep"), axis=1, tiled=True)
-    pieces = shard_piece.shape[1] // col_width
-    shaped = shard_piece.reshape(shard_piece.shape[0], pieces, col_width)
-    approx = jnp.einsum("td,dsc->tsc", attn_low, shaped, preferred_element_type=jnp.float32)
+    shaped = gather_columns(
+        projection, mesh.shape["grp"], mesh.shape["rep"], mesh.shape["tp"]
+    )
+    pieces = shaped.shape[0]
+    approx = jnp.einsum("td,sdc->tsc", attn_low, shaped, preferred_element_type=jnp.float32)
     code_rows = slab_codes[0].astype(jnp.float32)
     scale_rows = slab_scales[0].astype(jnp.float32)
     target = (code_rows.reshape(rows_dev, -1, QBLOCK) * scale_rows[..., None]).reshape(
@@ -91,7 +227,7 @@
     )
     errors = (approx - target).astype(jnp.bfloat16)
     partial_terms = jnp.einsum(
-        "tsc,dsc->std", errors, shaped, preferred_element_type=jnp.float32
+        "tsc,sdc->std", errors, shaped, preferred_element_type=jnp.float32
     ).astype(jnp.bfloat16)
     grad_attn = partial_terms.astype(jnp.float32).sum(0)
     grad_low = grad_attn.astype(jnp.bfloat16)
@@ -129,14 +265,11 @@
     )
     key_terms = grad_keys.transpose(1, 0, 2).reshape(1, length, KV_HEADS * HEAD_DIM)
     value_terms = grad_values.transpose(1, 0, 2).reshape(1, length, KV_HEADS * HEAD_DIM)
-    key_grad, value_grad = (
-        lax.psum_scatter(
-            key_terms.astype(jnp.bfloat16), ("grp", "rep"), scatter_dimension=1, tiled=True
-        ).astype(jnp.float32),
-        lax.psum_scatter(
-            value_terms.astype(jnp.bfloat16), ("grp", "rep"), scatter_dimension=1, tiled=True
-        ).astype(jnp.float32),
-    )
+    pair_terms = jnp.concatenate([key_terms, value_terms], 2).astype(jnp.bfloat16)
+    pair_grad = lax.psum_scatter(
+        pair_terms, ("grp", "rep"), scatter_dimension=1, tiled=True
+    )
+    key_grad, value_grad = pair_grad[..., :kv_width], pair_grad[..., kv_width:]
     query_grad = (
         grad_queries.transpose(2, 0, 1, 3)
         .reshape(1, rows_dev, HEADS * HEAD_DIM)
@@ -155,7 +288,7 @@
         P(None, ("grp", "rep")),
     )
     return jax.shard_map(
-        shards,
+        functools.partial(shards, mesh),
         mesh=mesh,
         in_specs=placed,
         out_specs=(

time: 328 us -> 241 us (0.73)
  waiting for transfers between devices: 221 us -> 39.5 us
  Pallas kernels: 0 us -> 90.6 us
  other arithmetic: 7.09 us -> 11 us
    all_gather x3 -> x1, waiting for transfers between devices: 150 us -> 0.01 us  [shards(): lax.all_gather(jnp.concatenate([key_rows, value_rows], 2), ('grp', 'rep')...]
    pallas_call x0 -> x1, Pallas kernels: none -> 90.6 us  [gather_columns(): pl.pallas_call(functools.partial(gather_kernel, n_grp), out_shape=jax.Sha...]
    reduce_scatter x2 -> x1, waiting for transfers between devices: 59.4 us -> 37.1 us  [shards(): lax.psum_scatter(pair_terms, ('grp', 'rep'), scatter_dimension=1, tiled=T...]
    all_to_all x1, waiting for transfers between devices: 9.92 us -> 0.01 us  [shards(): lax.all_to_all(teacher_codes, 'tp', split_axis=0, concat_axis=2, tiled=True)]
    convert_element_type x4 -> x0, local copies, waits for them, and re-layouts: 6.52 us -> none  [the longest x2 3.28 us: shards(): value_terms.astype(jnp.bfloat16)]
    unnamed x15 -> x12, local copies, waits for them, and re-layouts: 14.7 us -> 9.49 us
    slice x0 -> x2, local copies, waits for them, and re-layouts: none -> 4.39 us  [the longest x1 2.7 us: shards(): pairs_all[..., kv_width:]]
    transpose x0 -> x2, local copies, waits for them, and re-layouts: none -> 4.07 us  [the longest x1 2.04 us: shards(): grad_keys.transpose(1, 0, 2).reshape(1, length, KV_HEADS * HEAD_DIM)]
  transfers between devices with their start and end apart: 7 -> 4, of which waited for: 6 -> 2; matrix products, arithmetic and copies ran while one was open for 11% -> 4% of each run, Pallas kernels for 0% -> 38%
where the time goes in v1:
time: 241 us; the launch traced here: 240 us
  Pallas kernels  90.6 us (38%)
  matrix products  42 us (17%)
  waiting for transfers between devices  39.5 us (16%)
  local copies, waits for them, and re-layouts  33.5 us (14%)
  between operations  14.2 us (6%)
  other arithmetic  11 us (5%)
  starting transfers between devices  9.53 us (4%)
    pallas_call x1, Pallas kernels, gather_columns(): pl.pallas_call(functools.partial(gather_kernel, n_grp), out_shape=jax.Sha...  90.6 us
    reduce_scatter x1, waiting for transfers between devices, shards(): lax.psum_scatter(pair_terms, ('grp', 'rep'), scatter_dimension=1, tiled=T...  37.1 us
    dot_general x1, matrix products, shards(): jnp.einsum('tsc,sdc->std', errors, shaped, preferred_element_type=jnp.flo...  24.1 us
    unnamed x12, local copies, waits for them, and re-layouts  9.49 us
    dot_general x1, matrix products, output_step(): jnp.einsum('hgqk,hkd->hgqd', prob_low, value_part, preferred_element_type...  5.58 us
    all_to_all x1, starting transfers between devices, shards(): lax.all_to_all(teacher_scales, 'tp', split_axis=0, concat_axis=2, tiled=T...  5.2 us
  transfers between devices with their start and end apart: 4, of which 2 were waited for; matrix products, arithmetic and copies ran while one was open for 4% of the time, Pallas kernels for 38%

profile of v1, /device:TPU:0, one launch (start us, length us, event | category | flops | bytes accessed | tf_op | source)
XLA Modules:
  0.0 240.5 jit_solution(4283618868434209364)
XLA Ops:
  10.0 5.2 %all-to-all-start.1 = ((bf16[4,128,8]{1,2,0:T(8,128)(2,1)}), bf16[4,128,8]{1,2,0:T(8,128)(2,1)S(1)}, u32[]{:S(2)}, u32[]{:S(2)}) async-start(bf16[4,128,8]{1,2,0:T(8,128)(2,1)} %param.16), calls=%async_computation.1 | async-start | bytes 16384 | tf_op jit(solution)/shard_map/all_to_all | solution.py:171
  15.2 2.3 copy.48
  17.5 2.4 %all-to-all-done.1 = bf16[4,128,8]{1,2,0:T(8,128)(2,1)S(1)} async-done(((bf16[4,128,8]{1,2,0:T(8,128)(2,1)}), bf16[4,128,8]{1,2,0:T(8,128)(2,1)S(1)}, u32[]{:S(2)}, u32[]{:S(2)}) %all-to-all-start.1) | async-done | bytes 8224 | tf_op jit(solution)/shard_map/all_to_all | solution.py:171
  19.9 4.2 %all-to-all-start = ((bf16[4,128,1024]{1,2,0:T(8,128)(2,1)}), bf16[4,128,1024]{1,2,0:T(8,128)(2,1)}, u32[]{:S(2)}, u32[]{:S(2)}) async-start(bf16[4,128,1024]{1,2,0:T(8,128)(2,1)} %copy.48), calls=%async_computation | async-start | bytes 2097152 | tf_op jit(solution)/shard_map/all_to_all | solution.py:170
  25.8 90.6 %shard_map.85 = bf16[8,2048,512]{2,1,0:T(8,128)(2,1)} custom-call(bf16[2048,512]{1,0:T(8,128)(2,1)} %own_ref.1), custom_call_target="tpu_custom_call" | custom-call | bytes 100663296 | tf_op jit(solution)/shard_map/pallas_call | solution.py:140
  116.6 1.9 copy.50
  119.8 1.8 copy.49
  121.6 2.7 %fusion.26 = (bf16[1,1024,512]{1,2,0:T(8,128)(2,1)}, bf16[1,1024,512]{1,2,0:T(8,128)(2,1)S(1)}) fusion(bf16[1,1024,1024]{1,2,0:T(8,128)(2,1)} %all-gather.2.cloned.1.call-done), kind=kLoop, calls=%fused_computation.46 | loop fusion | bytes 4194304 | tf_op jit(solution)/shard_map/slice | solution.py:159
  125.0 4.2 %while.39 = (s32[]{:T(128)}, f32[4,4,128]{2,1,0:T(4,128)S(1)}, f32[4,4,128]{2,1,0:T(4,128)S(1)}, s32[]{:T(128)}, bf16[4,4,128,128]{3,2,1,0:T(8,128)(2,1)S(1)}, /...) while((s32[]{:T(128)}, f32[4,4,128]{2,1,0:T(4,128)S(1)}, ...), condition=%wide.region_3.4_spmd.clone, body=%wide.region_0.3_spmd.clone.sunk | while | flops 551687296 | bytes 18859120 | solution.py:194
  126.8 2.3 exponential_reduce_fusion.2
  129.2 1.6 copy.45
  131.9 5.7 %while.40 = (s32[]{:T(128)}, f32[4,4,128,128]{3,2,1,0:T(8,128)}, s32[]{:T(128)}, bf16[4,4,128,128]{3,2,1,0:T(8,128)(2,1)S(1)}, bf16[4,1024,128]{2,1,0:T(8,128)(2...) while((s32[]{:T(128)}, f32[4,4,128,128]{3,2,1,0:T(8,128)}, ...), condition=%wide.region_5.6_spmd.clone, body=%wide.region_4.5_spmd.clone.sunk | while | flops 1084621952 | bytes 5006465 | solution.py:211
  132.1 5.6 %fusion.70 = f32[4,4,128,128]{3,2,1,0:T(8,128)} fusion(f32[4,4,128,128]{3,2,1,0:T(8,128)} %get-tuple-element.573, f32[4,4,128]{2,1,0:T(4,128)S(1)} %get-tuple-element.589, f32[4,4,128]{2,1,0:T(4,128)S(1)} %get-tuple-element.588, pred[128,1024]{1,0:T(8,128)(4,1)S(1)} %broadcast_compare_fusion.7, bf16[4,4,128,128]{3,2,1,0:T(8,128)(2,1)S(1)} %get-tuple-element.586, ...), kind=kOutput, calls=%fused_computation.15.clone.1 | convolution fusion | flops 1084489728 | bytes 4866048 | tf_op jit(solution)/shard_map/while/body/hgqk,hkd->hgqd/dot_general | solution.py:207
  137.7 2.9 %copy.46 = f32[4,4,128,128]{2,3,1,0:T(8,128)} copy(f32[4,4,128,128]{3,2,1,0:T(8,128)} %get-tuple-element.160) | data formatting | bytes 2097152 | tf_op jit(solution)/shard_map/while | solution.py:211
  141.9 24.1 %convert_reduce_fusion = bf16[128,2048]{1,0:T(8,128)(2,1)} fusion(bf16[8,2048,512]{2,1,0:T(8,128)(2,1)} %shard_map.85, f32[128,8,512]{2,0,1:T(8,128)} %copy.49, f32[128,8,512]{2,0,1:T(8,128)} %copy.50, bf16[128,2048,1]{0,1,2:T(8,128)(2,1)S(1)} %bitcast.145), kind=kOutput, calls=%fused_computation.36 | convolution fusion | flops 4300472320 | bytes 22020096 | tf_op jit(solution)/shard_map/tsc,sdc->std/dot_general | solution.py:229
  172.6 11.0 %while.41 = (s32[]{:T(128)}, f32[4,4,128,128]{3,2,1,0:T(8,128)S(1)}, bf16[4,1024,128]{2,1,0:T(8,128)(2,1)}, bf16[4,1024,128]{2,1,0:T(8,128)(2,1)}, s32[]{:T(128)...) while((s32[]{:T(128)}, ...), condition=%wide.region_9.10_spmd.clone, body=%wide.region_8.9_spmd.clone.sunk | while | flops 2703623168 | bytes 51676348 | solution.py:260
  172.7 2.8 %exponential_divide_fusion.2 = f32[4,4,128,1024]{3,2,1,0:T(8,128)S(1)} fusion(f32[4,4,128]{2,1,0:T(4,128)S(1)} %get-tuple-element.632, f32[4,4,128]{2,1,0:T(4,128)S(1)} %get-tuple-element.631, pred[128,1024]{1,0:T(8,128)(4,1)S(1)} %broadcast_compare_fusion.8, bf16[4,4,128,128]{3,2,1,0:T(8,128)(2,1)S(1)} %get-tuple-element.629, ...), kind=kOutput, calls=%fused_computation.24.clone.1 | convolution fusion | flops 545259520 | bytes 10108928 | tf_op jit(solution)/shard_map/while/body/hgqd,hkd->hgqk/dot_general | solution.py:177
  178.3 2.6 %convolution_bitcast_fusion.2 = bf16[4,1024,128]{2,1,0:T(8,128)(2,1)} fusion(bf16[4,4,128,1024]{3,2,1,0:T(8,128)(2,1)S(1)} %multiply_convert_fusion.2, bf16[4,4,128,128]{3,2,1,0:T(8,128)(2,1)S(1)} %get-tuple-element.629), kind=kOutput, calls=%fused_computation.28.clone.1 | convolution fusion | flops 536870912 | bytes 5767168 | tf_op jit(solution)/shard_map/while/body/hgqk,hgqd->hkd/dot_general | solution.py:249
  180.9 2.6 %fusion.81 = bf16[4,1024,128]{2,1,0:T(8,128)(2,1)} fusion(bf16[4,4,128,128]{3,2,1,0:T(8,128)(2,1)S(1)} %get-tuple-element.633, f32[4,4,128,1024]{3,2,1,0:T(8,128)S(1)} %exponential_divide_fusion.2), kind=kOutput, calls=%fused_computation.27.clone.1 | convolution fusion | flops 538968064 | bytes 9961472 | tf_op jit(solution)/shard_map/while/body/hgqk,hgqd->hkd/dot_general | solution.py:252
  183.5 2.0 copy.58
  186.8 2.0 copy.59
  190.1 3.1 %pad_maximum_fusion = bf16[1,1024,1024]{2,1,0:T(8,128)(2,1)} fusion(bf16[1,1024,512]{2,1,0:T(8,128)(2,1)} %concatenate.21, bf16[1,1024,512]{2,1,0:T(8,128)(2,1)} %concatenate.20), kind=kLoop, calls=%fused_computation.37 | loop fusion | flops 4194304 | bytes 4194304 | tf_op jit(solution)/shard_map/concatenate | solution.py:268
  194.9 37.1 %reduce-scatter.2.cloned.1.call-done = bf16[1,128,1024]{2,1,0:T(8,128)(2,1)} async-done(((bf16[1,1024,1024]{2,1,0:T(8,128)(2,1)}), bf16[1,128,1024]{2,1,0:T(8,128)(2,1)}) %reduce-scatter.2.cloned.1.call-update) | async-done | bytes 262160 | tf_op jit(solution)/shard_map/reduce_scatter | solution.py:269
  232.0 1.7 fusion.27
  (51 shorter events, 24.6 us)
Async XLA Ops:
  7.2 114.5 %all-gather.2.cloned.1.call-start = ((), (), s32[]{:S(2)}) async-start(), calls=%async_computation.3 | async-start | bytes 2359296 | tf_op jit(solution)/shard_map/all_gather | solution.py:156
  10.0 9.9 %all-to-all-start.1 = ((bf16[4,128,8]{1,2,0:T(8,128)(2,1)}), bf16[4,128,8]{1,2,0:T(8,128)(2,1)S(1)}, u32[]{:S(2)}, u32[]{:S(2)}) async-start(bf16[4,128,8]{1,2,0:T(8,128)(2,1)} %param.16), calls=%async_computation.1 | async-start | bytes 16384 | tf_op jit(solution)/shard_map/all_to_all | solution.py:171
  19.9 98.5 %all-to-all-start = ((bf16[4,128,1024]{1,2,0:T(8,128)(2,1)}), bf16[4,128,1024]{1,2,0:T(8,128)(2,1)}, u32[]{:S(2)}, u32[]{:S(2)}) async-start(bf16[4,128,1024]{1,2,0:T(8,128)(2,1)} %copy.48), calls=%async_computation | async-start | bytes 2097152 | tf_op jit(solution)/shard_map/all_to_all | solution.py:170
  24.2 207.8 %reduce-scatter.2.cloned.1.call-start = ((), (), s32[]{:S(2)}) async-start(), calls=%async_computation.4 | async-start | bytes 2359296 | tf_op jit(solution)/shard_map/reduce_scatter | solution.py:269
  137.6 28.4 %copy-start = (bf16[4,1024,128]{2,1,0:T(8,128)(2,1)}, bf16[4,1024,128]{2,1,0:T(8,128)(2,1)S(1)}, u32[]{:S(2)}) copy-start(bf16[4,1024,128]{2,1,0:T(8,128)(2,1)S(1)} %get-tuple-element.645) | copy-start | bytes 3145732
  167.3 1.6 copy-start.2
  172.7 2.8 %copy-start.1 = (bf16[4,1024,128]{2,1,0:T(8,128)(2,1)S(1)}, bf16[4,1024,128]{2,1,0:T(8,128)(2,1)}, u32[]{:S(2)}) copy-start(bf16[4,1024,128]{2,1,0:T(8,128)(2,1)} %get-tuple-element.634) | copy-start | bytes 3145732 | tf_op jit(solution)/shard_map/while
Sparse Core Ops, SparseCore 0:
  10.1 51.8 all-gather.1
  193.3 38.5 reduce-scatter.1

commit v2 on v1

--- a/solution.py
+++ b/solution.py
@@ -95,11 +95,11 @@
 
     def on_xy(k, c):
         forward(k, c, qx, xs, sem_at(k, c), to_x).wait_recv()
-        if c % 2 == 0:
+        if events.index((k, c)) % 2 == 0:
             go(forward(k, c, qx, ds, sem_at(k, c), to_y))
         swap(k, c, qx, 1)
         forward(k, c, qy, ys, sem_at(k, c), to_y).wait_recv()
-        if c % 2 == 1:
+        if events.index((k, c)) % 2 == 1:
             go(forward(k, c, qy, ds, sem_at(k, c), to_x))
         swap(k, c, qy, 2)
 
@@ -158,10 +158,8 @@
     )
     keys_all, values_all = pairs_all[..., :kv_width], pairs_all[..., kv_width:]
     length = keys_all.shape[1]
-    key_block = min(1024, length)
     my_index = lax.axis_index(("grp", "rep"))
     first_row = my_index * rows_dev
-    needed = (first_row + rows_dev + key_block - 1) // key_block
     queries = query_rows[0].reshape(rows_dev, KV_HEADS, group_size, HEAD_DIM).transpose(1, 2, 0, 3)
     key_heads = keys_all[0].reshape(length, KV_HEADS, HEAD_DIM).transpose(1, 0, 2)
     value_heads = values_all[0].reshape(length, KV_HEADS, HEAD_DIM).transpose(1, 0, 2)
@@ -171,45 +169,18 @@
         lax.all_to_all(teacher_scales, "tp", split_axis=0, concat_axis=2, tiled=True),
     )
 
-    def block_scores(block_index):
-        offset = block_index * key_block
-        raw_scores = (
-            jnp.einsum("hgqd,hkd->hgqk", queries, key_heads, preferred_element_type=jnp.float32)
-            * inv_root
-        )
-        col_pos = offset + jnp.arange(key_block, dtype=jnp.int32)
-        allowed = col_pos[None, :] <= row_pos[:, None]
-        return (jnp.where(allowed, raw_scores, masked_low), key_heads, value_heads)
-
-    def stats_step(block_index, running):
-        row_peak, row_total = running
-        scores, key_part, value_part = block_scores(block_index)
-        new_peak = jnp.maximum(row_peak, scores.max(-1))
-        row_total = row_total * jnp.exp(row_peak - new_peak) + jnp.exp(
-            scores - new_peak[..., None]
-        ).sum(-1)
-        return (new_peak, row_total)
-
-    stat_shape = (KV_HEADS, group_size, rows_dev)
-    row_peak, row_total = lax.fori_loop(
-        0,
-        needed,
-        stats_step,
-        (jnp.full(stat_shape, masked_low, jnp.float32), jnp.zeros(stat_shape, jnp.float32)),
-    )
-
-    def block_probs(scores):
-        return jnp.exp(scores - row_peak[..., None]) / row_total[..., None]
-
-    def output_step(block_index, running):
-        scores, key_part, value_part = block_scores(block_index)
-        prob_low = block_probs(scores).astype(jnp.bfloat16)
-        return running + jnp.einsum(
-            "hgqk,hkd->hgqd", prob_low, value_part, preferred_element_type=jnp.float32
-        )
-
-    attn_wide = lax.fori_loop(
-        0, needed, output_step, jnp.zeros((KV_HEADS, group_size, rows_dev, HEAD_DIM), jnp.float32)
+    raw_scores = (
+        jnp.einsum("hgqd,hkd->hgqk", queries, key_heads, preferred_element_type=jnp.float32)
+        * inv_root
+    )
+    allowed = jnp.arange(length, dtype=jnp.int32)[None, :] <= row_pos[:, None]
+    scores = jnp.where(allowed, raw_scores, masked_low)
+    row_peak = scores.max(-1, keepdims=True)
+    shifted = jnp.exp(scores - row_peak)
+    probs = shifted / shifted.sum(-1, keepdims=True)
+    prob_low = probs.astype(jnp.bfloat16)
+    attn_wide = jnp.einsum(
+        "hgqk,hkd->hgqd", prob_low, value_heads, preferred_element_type=jnp.float32
     )
     attn_low = (
         attn_wide.transpose(2, 0, 1, 3).reshape(rows_dev, HEADS * HEAD_DIM).astype(jnp.bfloat16)
@@ -234,34 +205,18 @@
     grad_heads = grad_low.reshape(rows_dev, KV_HEADS, group_size, HEAD_DIM).transpose(1, 2, 0, 3)
     row_delta = (grad_heads.astype(jnp.float32) * attn_wide).sum(-1)
 
-    def back_step(block_index, running):
-        grad_queries, grad_keys, grad_values = running
-        scores, key_part, value_part = block_scores(block_index)
-        probs = block_probs(scores)
-        prob_low = probs.astype(jnp.bfloat16)
-        grad_prob = jnp.einsum(
-            "hgqd,hkd->hgqk", grad_heads, value_part, preferred_element_type=jnp.float32
-        )
-        grad_score = (probs * (grad_prob - row_delta[..., None]) * inv_root).astype(jnp.bfloat16)
-        grad_queries = grad_queries + jnp.einsum(
-            "hgqk,hkd->hgqd", grad_score, key_part, preferred_element_type=jnp.float32
-        )
-        key_piece = jnp.einsum(
-            "hgqk,hgqd->hkd", grad_score, queries, preferred_element_type=jnp.float32
-        )
-        value_piece = jnp.einsum(
-            "hgqk,hgqd->hkd", prob_low, grad_heads, preferred_element_type=jnp.float32
-        )
-        grad_keys = key_piece
-        grad_values = value_piece
-        return (grad_queries, grad_keys, grad_values)
-
-    zeros_kv = jnp.zeros((KV_HEADS, length, HEAD_DIM), jnp.float32)
-    grad_queries, grad_keys, grad_values = lax.fori_loop(
-        0,
-        needed,
-        back_step,
-        (jnp.zeros((KV_HEADS, group_size, rows_dev, HEAD_DIM), jnp.float32), zeros_kv, zeros_kv),
+    grad_values = jnp.einsum(
+        "hgqk,hgqd->hkd", prob_low, grad_heads, preferred_element_type=jnp.float32
+    )
+    grad_prob = jnp.einsum(
+        "hgqd,hkd->hgqk", grad_heads, value_heads, preferred_element_type=jnp.float32
+    )
+    grad_score = (probs * (grad_prob - row_delta[..., None]) * inv_root).astype(jnp.bfloat16)
+    grad_queries = jnp.einsum(
+        "hgqk,hkd->hgqd", grad_score, key_heads, preferred_element_type=jnp.float32
+    )
+    grad_keys = jnp.einsum(
+        "hgqk,hgqd->hkd", grad_score, queries, preferred_element_type=jnp.float32
     )
     key_terms = grad_keys.transpose(1, 0, 2).reshape(1, length, KV_HEADS * HEAD_DIM)
     value_terms = grad_values.transpose(1, 0, 2).reshape(1, length, KV_HEADS * HEAD_DIM)

time: 241 us -> 231 us (0.959)
  local copies, waits for them, and re-layouts: 33.5 us -> 23.9 us
  matrix products: 42 us -> 45.7 us
  Pallas kernels: 90.6 us -> 87.2 us
    sub x0 -> x1, matrix products: none -> 7.26 us  [shards(): shifted = jnp.exp(scores - row_peak)]
    transpose x2 -> x0, local copies, waits for them, and re-layouts: 4.07 us -> none  [the longest x1 2.04 us: shards(): grad_keys.transpose(1, 0, 2).reshape(1, length, KV_HEADS * HEAD_DIM)]
    pallas_call x1, Pallas kernels: 90.6 us -> 87.2 us  [gather_columns(): pl.pallas_call(functools.partial(gather_kernel, n_grp), out_shape=jax.Sha...]
    convert_element_type x2 -> x1, other arithmetic: 1.4 us -> 4.48 us  [shards(): prob_low = probs.astype(jnp.bfloat16)]
    dot_general x7 -> x5, matrix products: 17.9 us -> 14.9 us  [the longest x1 4.78 us: shards(): jnp.einsum('hgqd,hkd->hgqk', grad_heads, value_heads, preferred_element_t...]
    while x4 -> x0, local copies, waits for them, and re-layouts: 2.95 us -> none  [the longest x1 2.95 us: shards(): lax.fori_loop(0, needed, output_step, jnp.zeros((KV_HEADS, group_size, ro...]
    unnamed x12 -> x16, local copies, waits for them, and re-layouts: 9.49 us -> 7.78 us
  transfers between devices with their start and end apart: 4 -> 4, of which waited for: 2 -> 2; matrix products, arithmetic and copies ran while one was open for 4% -> 7% of each run, Pallas kernels for 38% -> 38%
where the time goes in v2:
time: 231 us
  Pallas kernels  87.2 us (38%)
  matrix products  45.7 us (20%)
  waiting for transfers between devices  39.7 us (17%)
  local copies, waits for them, and re-layouts  23.9 us (10%)
  between operations  14.2 us (6%)
  other arithmetic  11 us (5%)
  starting transfers between devices  8.8 us (4%)
    pallas_call x1, Pallas kernels, gather_columns(): pl.pallas_call(functools.partial(gather_kernel, n_grp), out_shape=jax.Sha...  87.2 us
    reduce_scatter x1, waiting for transfers between devices, shards(): lax.psum_scatter(pair_terms, ('grp', 'rep'), scatter_dimension=1, tiled=T...  37.2 us
    dot_general x1, matrix products, shards(): jnp.einsum('tsc,sdc->std', errors, shaped, preferred_element_type=jnp.flo...  23.6 us
    unnamed x16, local copies, waits for them, and re-layouts  7.78 us
    sub x1, matrix products, shards(): shifted = jnp.exp(scores - row_peak)  7.26 us
    all_to_all x1, starting transfers between devices, shards(): lax.all_to_all(teacher_scales, 'tp', split_axis=0, concat_axis=2, tiled=T...  5.2 us
    dot_general x1, matrix products, shards(): jnp.einsum('hgqd,hkd->hgqk', grad_heads, value_heads, preferred_element_t...  4.78 us
  transfers between devices with their start and end apart: 4, of which 2 were waited for; matrix products, arithmetic and copies ran while one was open for 7% of the time, Pallas kernels for 38%

profile of v2, /device:TPU:0, one launch (start us, length us, event | category | flops | bytes accessed | tf_op | source)
XLA Modules:
  0.0 230.5 jit_solution(67321459751837159)
XLA Ops:
  10.1 5.2 %all-to-all-start.1 = ((bf16[4,128,8]{1,2,0:T(8,128)(2,1)}), bf16[4,128,8]{1,2,0:T(8,128)(2,1)S(1)}, u32[]{:S(2)}, u32[]{:S(2)}) async-start(bf16[4,128,8]{1,2,0:T(8,128)(2,1)} %param.10), calls=%async_computation.1 | async-start | bytes 16384 | tf_op jit(solution)/shard_map/all_to_all | solution.py:169
  15.3 2.3 copy.49
  17.5 2.4 %all-to-all-done.1 = bf16[4,128,8]{1,2,0:T(8,128)(2,1)S(1)} async-done(((bf16[4,128,8]{1,2,0:T(8,128)(2,1)}), bf16[4,128,8]{1,2,0:T(8,128)(2,1)S(1)}, u32[]{:S(2)}, u32[]{:S(2)}) %all-to-all-start.1) | async-done | bytes 8224 | tf_op jit(solution)/shard_map/all_to_all | solution.py:169
  20.0 3.5 %all-to-all-start = ((bf16[4,128,1024]{1,2,0:T(8,128)(2,1)}), bf16[4,128,1024]{1,2,0:T(8,128)(2,1)S(1)}, u32[]{:S(2)}, u32[]{:S(2)}) async-start(bf16[4,128,1024]{1,2,0:T(8,128)(2,1)} %copy.49), calls=%async_computation | async-start | bytes 2097152 | tf_op jit(solution)/shard_map/all_to_all | solution.py:168
  24.6 87.2 %shard_map.85 = bf16[8,2048,512]{2,1,0:T(8,128)(2,1)} custom-call(bf16[2048,512]{1,0:T(8,128)(2,1)} %own_ref.1), custom_call_target="tpu_custom_call" | custom-call | bytes 100663296 | tf_op jit(solution)/shard_map/pallas_call | solution.py:140
  111.9 1.4 mul.36
  113.3 1.9 copy.51
  115.3 1.4 bitcast_convert_fusion.2
  116.7 2.9 %copy.50 = f32[128,8,512]{2,0,1:T(8,128)} copy(f32[128,8,512]{0,2,1:T(8,128)} %bitcast.113) | data formatting | bytes 4194304 | tf_op jit(solution)/shard_map/convert_element_type | solution.py:194
  119.6 2.7 %fusion.17 = (bf16[1,1024,512]{1,2,0:T(8,128)(2,1)}, bf16[1,1024,512]{1,2,0:T(8,128)(2,1)S(1)}) fusion(bf16[1,1024,1024]{1,2,0:T(8,128)(2,1)} %all-gather.2.cloned.1.call-done), kind=kLoop, calls=%fused_computation.28 | loop fusion | bytes 4194304 | tf_op jit(solution)/shard_map/slice | solution.py:159
  122.3 1.3 copy.44
  123.7 7.3 %fusion.19 = (f32[4,4,128]{2,1,0:T(4,128)S(1)}, f32[4,4,128,1024]{2,3,1,0:T(8,128)}) fusion(pred[128,1024]{0,1:T(8,128)(4,1)S(1)} %iota_compare_fusion, bf16[4,4,128,128]{2,3,1,0:T(8,128)(2,1)} %bitcast.121, bf16[1024,4,128]{2,0,1:T(8,128)(2,1)} %copy.44), kind=kOutput, calls=%fused_computation.30 | convolution fusion | flops 545260544 | bytes 10100736 | tf_op jit(solution)/shard_map/sub | solution.py:179
  130.9 4.5 %fusion.5 = bf16[4,4,128,1024]{2,3,1,0:T(8,128)(2,1)S(1)} fusion(f32[4,4,128,1024]{2,3,1,0:T(8,128)} %get-tuple-element.17, f32[4,4,128]{2,1,0:T(4,128)S(1)} %get-tuple-element.16), kind=kLoop, calls=%fused_computation.10 | loop fusion | flops 4194304 | bytes 12591104 | tf_op jit(solution)/shard_map/convert_element_type | solution.py:181
  135.4 1.9 copy-done
  137.4 1.9 fusion.24
  139.3 23.6 %convert_reduce_fusion = bf16[128,2048]{1,0:T(8,128)(2,1)} fusion(bf16[8,2048,512]{2,1,0:T(8,128)(2,1)} %shard_map.85, f32[128,8,512]{2,0,1:T(8,128)} %copy.50, f32[128,8,512]{2,0,1:T(8,128)S(1)} %copy.51, bf16[128,2048,1]{0,1,2:T(8,128)(2,1)} %bitcast.118), kind=kOutput, calls=%fused_computation.5 | convolution fusion | flops 4300472320 | bytes 22020096 | tf_op jit(solution)/shard_map/tsc,sdc->std/dot_general | solution.py:200
  164.2 1.4 multiply_reduce_fusion
  165.6 3.8 %bitcast_convert_fusion = bf16[4,1024,128]{1,2,0:T(8,128)(2,1)S(1)} fusion(bf16[4,4,128,1024]{2,3,1,0:T(8,128)(2,1)} %copy-done, bf16[4,4,128,128]{2,3,1,0:T(8,128)(2,1)S(1)} %bitcast.116), kind=kOutput, calls=%fused_computation.13 | convolution fusion | flops 537395200 | bytes 5767168 | tf_op jit(solution)/shard_map/hgqk,hgqd->hkd/dot_general | solution.py:208
  169.3 4.8 %multiply_convert_fusion = bf16[4,4,128,1024]{2,3,1,0:T(8,128)(2,1)S(1)} fusion(f32[4,4,128]{2,1,0:T(4,128)S(1)} %multiply_reduce_fusion, f32[4,4,128,1024]{2,3,1,0:T(8,128)} %get-tuple-element.17, f32[4,4,128]{2,1,0:T(4,128)S(1)} %get-tuple-element.16, bf16[4,4,128,128]{2,3,1,0:T(8,128)(2,1)S(1)} %bitcast.117, bf16[4,1024,128,1]{1,2,3,0:T(8,128)(2,1)S(1)} %bitcast.120), kind=kOutput, calls=%fused_computation.2 | convolution fusion | flops 547356672 | bytes 14172160 | tf_op jit(solution)/shard_map/hgqd,hkd->hgqk/dot_general | solution.py:211
  174.1 1.5 bitcast_convert_fusion.1
  177.9 2.9 %pad_maximum_fusion = bf16[1,1024,1024]{2,1,0:T(8,128)(2,1)} fusion(bf16[1,1024,512]{2,1,0:T(8,128)(2,1)S(1)} %copy.61, bf16[1,1024,512]{2,1,0:T(8,128)(2,1)} %copy.60), kind=kLoop, calls=%fused_computation.12 | loop fusion | flops 4194304 | bytes 4194304 | tf_op jit(solution)/shard_map/concatenate | solution.py:223
  180.8 2.9 %convolution_convert_fusion = bf16[4,4,128,128]{2,3,1,0:T(8,128)(2,1)S(1)} fusion(bf16[4,1024,128,1]{1,2,3,0:T(8,128)(2,1)S(1)} %bitcast.111, bf16[4,4,128,1024]{2,3,1,0:T(8,128)(2,1)} %copy-done.1), kind=kOutput, calls=%fused_computation.16 | convolution fusion | flops 537133056 | bytes 5767168 | tf_op jit(solution)/shard_map/hgqk,hkd->hgqd/dot_general | solution.py:215
  184.8 37.2 %reduce-scatter.2.cloned.1.call-done = bf16[1,128,1024]{2,1,0:T(8,128)(2,1)} async-done(((bf16[1,1024,1024]{2,1,0:T(8,128)(2,1)}), bf16[1,128,1024]{2,1,0:T(8,128)(2,1)}) %reduce-scatter.2.cloned.1.call-update) | async-done | bytes 262160 | tf_op jit(solution)/shard_map/reduce_scatter | solution.py:224
  222.0 1.7 fusion.18
  (28 shorter events, 8.7 us)
Async XLA Ops:
  7.2 16.4 %copy-start.5 = (bf16[1,128,2048]{2,1,0:T(8,128)(2,1)S(1)}, bf16[1,128,2048]{2,1,0:T(8,128)(2,1)}, u32[]{:S(2)}) copy-start(bf16[1,128,2048]{2,1,0:T(8,128)(2,1)} %param.6) | copy-start | bytes 1572868
  7.2 112.4 %all-gather.2.cloned.1.call-start = ((), (), s32[]{:S(2)}) async-start(), calls=%async_computation.3 | async-start | bytes 2359296 | tf_op jit(solution)/shard_map/all_gather | solution.py:156
  10.1 9.9 %all-to-all-start.1 = ((bf16[4,128,8]{1,2,0:T(8,128)(2,1)}), bf16[4,128,8]{1,2,0:T(8,128)(2,1)S(1)}, u32[]{:S(2)}, u32[]{:S(2)}) async-start(bf16[4,128,8]{1,2,0:T(8,128)(2,1)} %param.10), calls=%async_computation.1 | async-start | bytes 16384 | tf_op jit(solution)/shard_map/all_to_all | solution.py:169
  20.0 95.3 %all-to-all-start = ((bf16[4,128,1024]{1,2,0:T(8,128)(2,1)}), bf16[4,128,1024]{1,2,0:T(8,128)(2,1)S(1)}, u32[]{:S(2)}, u32[]{:S(2)}) async-start(bf16[4,128,1024]{1,2,0:T(8,128)(2,1)} %copy.49), calls=%async_computation | async-start | bytes 2097152 | tf_op jit(solution)/shard_map/all_to_all | solution.py:168
  23.5 198.5 %reduce-scatter.2.cloned.1.call-start = ((), (), s32[]{:S(2)}) async-start(), calls=%async_computation.4 | async-start | bytes 2359296 | tf_op jit(solution)/shard_map/reduce_scatter | solution.py:224
  130.9 6.5 %copy-start.2 = (bf16[1,1024,512]{1,2,0:T(8,128)(2,1)S(1)}, bf16[1,1024,512]{1,2,0:T(8,128)(2,1)}, u32[]{:S(2)}) copy-start(bf16[1,1024,512]{1,2,0:T(8,128)(2,1)} %get-tuple-element.12) | copy-start | bytes 3145732
  135.4 2.0 copy-start
  165.5 3.8 %copy-start.3 = (bf16[1,1024,512]{1,2,0:T(8,128)(2,1)S(1)}, bf16[1,1024,512]{1,2,0:T(8,128)(2,1)}, u32[]{:S(2)}) copy-start(bf16[1,1024,512]{1,2,0:T(8,128)(2,1)} %get-tuple-element.12) | copy-start | bytes 3145732
  169.3 4.8 %copy-start.4 = (bf16[1,128,2048]{1,2,0:T(8,128)(2,1)S(1)}, bf16[1,128,2048]{1,2,0:T(8,128)(2,1)}, u32[]{:S(2)}) copy-start(bf16[1,128,2048]{1,2,0:T(8,128)(2,1)} %copy.77) | copy-start | bytes 1572868
  174.1 1.9 copy-start.1
Sparse Core Ops, SparseCore 0:
  10.2 52.3 all-gather.1
  180.9 41.0 reduce-scatter.1
